TPU v7x, 32 devices: a whole 2x2x4 slice. The times are simulated.
32 devices in a mesh: patch: 16 (over z, y, x), pix: 2 (over core).
Axes of the slice: x: 2, y: 2, z: 4, core: 2. Of those that a mesh axis runs over, the one named last changes fastest.
Arguments:
- pixel_pos: float32 [2, 3072], P(None, ('patch', 'pix')), may hold values from -4 to 4
- pixel_view: float32 [3, 3072], P(None, ('patch', 'pix')), may hold values from -1 to 1
- observed: float32 [3072], P(('patch', 'pix')), may hold values from -6 to 6
- noise_scale: float32 [3072], P(('patch', 'pix')), may hold values from 0.5 to 2
- valid_mask: int32 [3072], P(('patch', 'pix')), may hold values 0 or 1
- patch_pos: float32 [2, 768], P(None, 'patch'), may hold values from -4 to 4
- patch_depth: float32 [768], P('patch'), may hold values from 0.3 to 1.5
- segment_ids: int32 [768], P('patch'), may hold values from 0 to 15, never falling along the last dimension, each value on 1 to 192 neighbouring positions
- seg_strike: float32 [16], replicated, may hold values from -3.140625 to 3.140625
- seg_dip: float32 [16], replicated, may hold values from 0.35 to 1.4
- slip_models: bfloat16 [768, 3, 128], P('patch'), may hold values from -0.8984375 to 0.8984375
Outputs:
- residual: float32 [3072, 128], P(('patch', 'pix'))
- misfit: float32 [128], replicated
Inputs may be any that keep to these rules, and one draw needn't show every extreme that they name: `segment_ids`: segment ids never fall along the patches.
All inputs are finite; a program needn't handle non-finite values. No bound on the sum of `valid_mask` on one device may be relied on, other than what follows from the above.
Results may differ from a plain program's by a relative error of at most 0.0003.
Values may be sent and summed in bfloat16 or wider, within the bound.
A program may use at most 64 MiB of HBM per device.

v0:
```python
import math
import jax
import jax.numpy as jnp
from jax import lax
from jax.sharding import PartitionSpec as P

two_pi = 2.0 * math.pi
mu_ratio = 0.5


def partner(value, axis, distance):
    mask = 2**distance
    pairs = [(source, source ^ mask) for source in range(lax.axis_size(axis))]
    return lax.ppermute(value, axis, pairs)


def point_green(pixel_pos, pixel_view, frame_rows):
    src_east = frame_rows[0][:, None]
    src_north = frame_rows[1][:, None]
    src_depth = frame_rows[2][:, None]
    sin_strike = frame_rows[3][:, None]
    cos_strike = frame_rows[4][:, None]
    sin_dip = frame_rows[5][:, None]
    cos_dip = frame_rows[6][:, None]
    east_gap = pixel_pos[0][None, :] - src_east
    north_gap = pixel_pos[1][None, :] - src_north
    along_x = east_gap * sin_strike + north_gap * cos_strike
    across = north_gap * sin_strike - east_gap * cos_strike
    depth_term = across * cos_dip + src_depth * sin_dip
    plane_term = across * sin_dip - src_depth * cos_dip
    radius = jnp.sqrt(along_x * along_x + across * across + src_depth * src_depth)
    over_r = 1.0 / radius
    over_r3 = over_r * over_r * over_r
    over_r5 = over_r3 * over_r * over_r
    over_rd = 1.0 / (radius + src_depth)
    base_term = over_r * over_rd * over_rd
    cubic_term = (3.0 * radius + src_depth) * over_r3 * over_rd * over_rd * over_rd
    square_term = (2.0 * radius + src_depth) * over_r3 * over_rd * over_rd
    term_one = mu_ratio * across * (base_term - along_x * along_x * cubic_term)
    term_two = mu_ratio * along_x * (base_term - across * across * cubic_term)
    term_three = mu_ratio * along_x * over_r3 - term_two
    term_four = -mu_ratio * along_x * across * square_term
    term_five = mu_ratio * (over_r * over_rd - along_x * along_x * square_term)
    scaled_q = 3.0 * plane_term * over_r5
    dip_mixed = sin_dip * cos_dip
    dip_square = sin_dip * sin_dip
    strike_x = -(scaled_q * along_x * along_x + term_one * sin_dip)
    strike_y = -(scaled_q * along_x * across + term_two * sin_dip)
    strike_z = -(scaled_q * along_x * src_depth + term_four * sin_dip)
    dip_x = -(scaled_q * along_x * depth_term - term_three * dip_mixed)
    dip_y = -(scaled_q * across * depth_term - term_one * dip_mixed)
    dip_z = -(scaled_q * src_depth * depth_term - term_five * dip_mixed)
    open_x = scaled_q * along_x * plane_term - term_three * dip_square
    open_y = scaled_q * across * plane_term - term_one * dip_square
    open_z = scaled_q * src_depth * plane_term - term_five * dip_square

    def project(comp_x, comp_y, comp_z):
        east_move = comp_x * sin_strike - comp_y * cos_strike
        north_move = comp_x * cos_strike + comp_y * sin_strike
        return (
            pixel_view[0][None, :] * east_move
            + pixel_view[1][None, :] * north_move
            + pixel_view[2][None, :] * comp_z
        ) / two_pi

    return jnp.stack(
        [
            project(strike_x, strike_y, strike_z),
            project(dip_x, dip_y, dip_z),
            project(open_x, open_y, open_z),
        ],
        axis=1,
    )


def local_frames(patch_pos, patch_depth, segment_ids, seg_strike, seg_dip):
    segment_count = seg_strike.shape[0]
    matches = segment_ids[:, None] == jnp.arange(segment_count, dtype=jnp.int32)[None, :]
    strike = jnp.sum(jnp.where(matches, seg_strike[None, :], 0.0), axis=1)
    dip_angle = jnp.sum(jnp.where(matches, seg_dip[None, :], 0.0), axis=1)
    return jnp.stack(
        [
            patch_pos[0],
            patch_pos[1],
            patch_depth,
            jnp.sin(strike),
            jnp.cos(strike),
            jnp.sin(dip_angle),
            jnp.cos(dip_angle),
        ],
        axis=0,
    )


def tile_product(site_pos, site_view, frame_rows, slip_table):
    pixel_count = site_pos.shape[1]
    green_tile = point_green(site_pos, site_view, frame_rows).astype(jnp.bfloat16)
    green_tile = green_tile.reshape(frame_rows.shape[1] * 3, pixel_count)
    return lax.dot_general(
        green_tile, slip_table, (((0,), (0,)), ((), ())), preferred_element_type=jnp.float32
    )


def patch_blocks(pixel_pos, pixel_view, frame_rows, slip_piece, running):
    patch_count = slip_piece.shape[0]
    samples = slip_piece.shape[2]
    block_len = min(patch_count, 640)
    full_blocks = patch_count // block_len
    remainder = patch_count - full_blocks * block_len
    head = full_blocks * block_len
    head_frames = frame_rows[:, :head].reshape(7, full_blocks, block_len).transpose(1, 0, 2)
    head_slip = slip_piece[:head].reshape(full_blocks, block_len * 3, samples)

    def add_tile(accum, block_items):
        return (accum + tile_product(pixel_pos, pixel_view, block_items[0], block_items[1]), None)

    running, _ = lax.scan(add_tile, running, (head_frames, head_slip))
    if remainder > 0:
        tail_slip = slip_piece[head:].reshape(remainder * 3, samples)
        running = running + tile_product(pixel_pos, pixel_view, frame_rows[:, head:], tail_slip)
    return running


def index_bit(level):
    return lax.axis_index("patch") // 2**level % 2 == 1


def join_pair(mine, other, upper, axis_dim):
    first = jnp.where(upper, other, mine)
    second = jnp.where(upper, mine, other)
    return jnp.concatenate([first, second], axis=axis_dim)


def per_device(
    pixel_pos,
    pixel_view,
    observed,
    noise_scale,
    valid_mask,
    patch_pos,
    patch_depth,
    segment_ids,
    seg_strike,
    seg_dip,
    slip_models,
):
    own_pixels = pixel_pos.shape[1]
    samples = slip_models.shape[2]
    frames = local_frames(patch_pos, patch_depth, segment_ids, seg_strike, seg_dip)
    total_bits = lax.axis_size("patch").bit_length() - 1
    low_count = (total_bits + 1) // 2
    group_slip = slip_models
    group_frames = frames
    for level in range(low_count):
        upper = index_bit(level)
        other_slip = partner(group_slip, "patch", level)
        other_frames = partner(group_frames, "patch", level)
        group_slip = join_pair(group_slip, other_slip, upper, 0)
        group_frames = join_pair(group_frames, other_frames, upper, 1)
    group_sites = jnp.concatenate([pixel_pos, pixel_view], axis=0)
    for level in range(low_count, total_bits):
        upper = index_bit(level)
        other_sites = partner(group_sites, "patch", level)
        group_sites = join_pair(group_sites, other_sites, upper, 1)
    site_groups = group_sites.shape[1] // own_pixels
    stacked = group_sites.reshape(5, site_groups, own_pixels).transpose(1, 0, 2)

    def one_group(block_sites):
        start = jnp.zeros((own_pixels, samples), jnp.float32)
        return patch_blocks(block_sites[:2], block_sites[2:], group_frames, group_slip, start)

    partial_value = lax.map(one_group, stacked).reshape(site_groups * own_pixels, samples)
    for level in range(total_bits - 1, low_count - 1, -1):
        upper = index_bit(level)
        half = partial_value.shape[0] // 2
        keep = jnp.where(upper, partial_value[half:], partial_value[:half])
        send = jnp.where(upper, partial_value[:half], partial_value[half:])
        partial_value = keep + partner(send, "patch", level)
    residual = (
        valid_mask.astype(jnp.float32)[:, None]
        * (partial_value - observed[:, None])
        / noise_scale[:, None]
    )
    own_sum = jnp.sum(residual * residual, axis=0)
    pixels = own_pixels * lax.axis_size("patch") * lax.axis_size("pix")
    misfit = lax.psum(own_sum, ("patch", "pix")) / pixels
    return (residual, misfit)


def solution(mesh):
    return jax.shard_map(
        per_device,
        mesh=mesh,
        in_specs=(
            P(None, ("patch", "pix")),
            P(None, ("patch", "pix")),
            P(("patch", "pix")),
            P(("patch", "pix")),
            P(("patch", "pix")),
            P(None, "patch"),
            P("patch"),
            P("patch"),
            P(),
            P(),
            P("patch", None, None),
        ),
        out_specs=(P(("patch", "pix"), None), P()),
        check_vma=False,
    )
```

profile of v0, /device:TPU:0, one launch (start us, length us, event | category | flops | bytes accessed | tf_op | source)
XLA Modules:
  0.0 74.1 jit_solution(12593632684655895281)
XLA Ops:
  0.6 3.0 %collective-permute-start.4 = (bf16[48,3,128]{2,0,1:T(8,128)(2,1)}, bf16[48,3,128]{2,0,1:T(8,128)(2,1)S(1)}, u32[]{:S(2)}, u32[]{:S(2)}) collective-permute-start(bf16[48,3,128]{2,0,1:T(8,128)(2,1)} %param.23), channel_id=1, source_target_pairs={{0,2},{2,0},{4,6},{6,4},{8,10},{10,8},{12,14},{14,12},{16,18},{18,... | collective-permute-start | bytes 110600 | tf_op jit(solution)/shard_map/ppermute | solution.py:14
  3.7 0.8 %select_reduce_fusion = (f32[48]{0:T(128)S(1)}, f32[48]{0:T(128)S(1)}) fusion(f32[16]{0:T(128)} %param.22, s32[48]{0:T(128)} %param.20, f32[16]{0:T(128)} %param.21), kind=kLoop, calls=%fused_computation.120 | loop fusion | flops 3744 | bytes 704 | tf_op jit(solution)/shard_map/reduce_sum | solution.py:80
  4.5 0.7 copy-done.3
  5.2 0.1 collective-permute-start.2
  5.3 0.6 copy-done.1
  5.9 1.6 %collective-permute-start = (f32[5,96]{1,0:T(8,128)S(1)}, f32[5,96]{1,0:T(8,128)S(1)}, u32[]{:S(2)}, u32[]{:S(2)}) collective-permute-start(f32[5,96]{1,0:T(8,128)S(1)} %pad_maximum_fusion.5), channel_id=1, source_target_pairs={{0,8},{2,10},{4,12},{6,14},{8,0},{10,2},{12,4},{14,6},{16,24},{18,... | collective-permute-start | bytes 5768 | tf_op jit(solution)/shard_map/ppermute | solution.py:14
  7.5 1.4 %collective-permute-done.2 = f32[7,48]{1,0:T(8,128)S(1)} collective-permute-done((f32[7,48]{1,0:T(8,128)S(1)}, f32[7,48]{1,0:T(8,128)S(1)}, u32[]{:S(2)}, u32[]{:S(2)}) %collective-permute-start.2) | collective-permute-done | bytes 1376 | tf_op jit(solution)/shard_map/ppermute | solution.py:14
  8.9 0.1 pad_maximum_fusion.6
  9.0 1.5 %collective-permute-start.3 = (f32[7,96]{1,0:T(8,128)S(1)}, f32[7,96]{1,0:T(8,128)S(1)}, u32[]{:S(2)}, u32[]{:S(2)}) collective-permute-start(f32[7,96]{1,0:T(8,128)S(1)} %pad_maximum_fusion.6), channel_id=1, source_target_pairs={{0,4},{2,6},{4,0},{6,2},{8,12},{10,14},{12,8},{14,10},{16,20},{18,... | collective-permute-start | bytes 8072 | tf_op jit(solution)/shard_map/ppermute | solution.py:14
  10.6 2.6 %collective-permute-start.1 = (f32[5,192]{1,0:T(8,128)S(1)}, f32[5,192]{1,0:T(8,128)S(1)}, u32[]{:S(2)}, u32[]{:S(2)}) collective-permute-start(f32[5,192]{1,0:T(8,128)S(1)} %pad_maximum_fusion.4), channel_id=1, source_target_pairs={{0,16},{2,18},{4,20},{6,22},{8,24},{10,26},{12,28},{14,30},{16,0},... | collective-permute-start | bytes 11528 | tf_op jit(solution)/shard_map/ppermute | solution.py:14
  13.2 0.1 multiply_bitcast_fusion
  13.3 0.1 multiply_bitcast_fusion.1
  13.5 1.6 %collective-permute-done.1 = f32[5,192]{1,0:T(8,128)S(1)} collective-permute-done((f32[5,192]{1,0:T(8,128)S(1)}, f32[5,192]{1,0:T(8,128)S(1)}, u32[]{:S(2)}, u32[]{:S(2)}) %collective-permute-start.1) | collective-permute-done | bytes 3872 | tf_op jit(solution)/shard_map/ppermute | solution.py:14
  15.2 0.7 collective-permute-start.5
  16.0 0.1 reshape.2726
  16.0 3.6 %collective-permute-done.5 = bf16[96,3,128]{2,0,1:T(8,128)(2,1)S(1)} collective-permute-done((bf16[96,3,128]{2,0,1:T(8,128)(2,1)S(1)}, bf16[96,3,128]{2,0,1:T(8,128)(2,1)S(1)}, u32[]{:S(2)}, u32[]{:S(2)}) %collective-permute-start.5) | collective-permute-done | bytes 73760 | tf_op jit(solution)/shard_map/ppermute | solution.py:14
  19.7 3.4 %while.11 = (s32[]{:T(128)}, f32[4,96,128]{2,1,0:T(8,128)S(1)}, f32[4,5,96]{2,0,1:T(4,128)S(1)}, f32[7,192]{1,0:T(8,128)S(1)}, f32[192,1]{0,1:T(1,128)S(1)}, /*i...) while((s32[]{:T(128)}, f32[4,96,128]{2,1,0:T(8,128)S(1)}, ...), condition=%wide.region_3.4_spmd, body=%wide.region_2.3_spmd.sunk | while | flops 16626054 | bytes 485213 | solution.py:172
  19.8 0.5 fusion.98
  20.3 0.2 fusion.99
  20.6 0.5 fusion.98
  21.2 0.2 fusion.99
  21.5 0.5 fusion.98
  22.0 0.2 fusion.99
  22.3 0.5 fusion.98
  22.9 0.2 fusion.99
  23.1 2.7 %collective-permute-start.6 = (f32[192,128]{1,0:T(8,128)S(1)}, f32[192,128]{1,0:T(8,128)S(1)}, u32[]{:S(2)}, u32[]{:S(2)}) collective-permute-start(f32[192,128]{1,0:T(8,128)S(1)} %bitcast.102), channel_id=1, source_target_pairs={{0,16},{2,18},{4,20},{6,22},{8,24},{10,26},{12,28},{14,30},{16,0},... | collective-permute-start | bytes 294920 | tf_op jit(solution)/shard_map/ppermute | solution.py:14
  25.8 2.9 %collective-permute-done.6 = f32[192,128]{1,0:T(8,128)S(1)} collective-permute-done((f32[192,128]{1,0:T(8,128)S(1)}, f32[192,128]{1,0:T(8,128)S(1)}, u32[]{:S(2)}, u32[]{:S(2)}) %collective-permute-start.6) | collective-permute-done | bytes 98336 | tf_op jit(solution)/shard_map/ppermute | solution.py:14
  28.8 2.2 %collective-permute-start.7 = (f32[96,128]{1,0:T(8,128)S(1)}, f32[96,128]{1,0:T(8,128)S(1)}, u32[]{:S(2)}, u32[]{:S(2)}) collective-permute-start(f32[96,128]{1,0:T(8,128)S(1)} %slice_select_fusion.2), channel_id=1, source_target_pairs={{0,8},{2,10},{4,12},{6,14},{8,0},{10,2},{12,4},{14,6},{16,24},{18,... | collective-permute-start | bytes 147464 | tf_op jit(solution)/shard_map/ppermute | solution.py:14
  31.0 2.1 %collective-permute-done.7 = f32[96,128]{1,0:T(8,128)S(1)} collective-permute-done((f32[96,128]{1,0:T(8,128)S(1)}, f32[96,128]{1,0:T(8,128)S(1)}, u32[]{:S(2)}, u32[]{:S(2)}) %collective-permute-start.7) | collective-permute-done | bytes 49184 | tf_op jit(solution)/shard_map/ppermute | solution.py:14
  33.0 0.7 multiply_reduce_fusion
  33.8 39.8 %psum.7 = f32[128]{0:T(128)S(1)} all-reduce(f32[128]{0:T(128)S(1)} %get-tuple-element.127), channel_id=1, replica_groups=mesh['patch'=16,'pix'=2] {'patch','pix'}, use_global_device_ids=true, to_apply=%region_5.6 | all-reduce | flops 128 | bytes 1024 | tf_op jit(solution)/shard_map/psum | solution.py:186
  73.6 0.5 broadcast_multiply_fusion.2
  (49 shorter events, 0.8 us)
Async XLA Ops:
  0.6 14.6 %collective-permute-start.4 = (bf16[48,3,128]{2,0,1:T(8,128)(2,1)}, bf16[48,3,128]{2,0,1:T(8,128)(2,1)S(1)}, u32[]{:S(2)}, u32[]{:S(2)}) collective-permute-start(bf16[48,3,128]{2,0,1:T(8,128)(2,1)} %param.23), channel_id=1, source_target_pairs={{0,2},{2,0},{4,6},{6,4},{8,10},{10,8},{12,14},{14,12},{16,18},{18,... | collective-permute-start | bytes 110600 | tf_op jit(solution)/shard_map/ppermute | solution.py:14
  4.5 0.7 copy-start.3
  4.5 0.7 copy-start.6
  5.2 0.7 copy-start.1
  5.2 0.7 copy-start.2
  5.2 3.7 %collective-permute-start.2 = (f32[7,48]{1,0:T(8,128)S(1)}, f32[7,48]{1,0:T(8,128)S(1)}, u32[]{:S(2)}, u32[]{:S(2)}) collective-permute-start(f32[7,48]{1,0:T(8,128)S(1)} %stack.24), channel_id=1, source_target_pairs={{0,2},{2,0},{4,6},{6,4},{8,10},{10,8},{12,14},{14,12},{16,18},{18,... | collective-permute-start | bytes 4040 | tf_op jit(solution)/shard_map/ppermute | solution.py:14
  5.9 4.6 %collective-permute-start = (f32[5,96]{1,0:T(8,128)S(1)}, f32[5,96]{1,0:T(8,128)S(1)}, u32[]{:S(2)}, u32[]{:S(2)}) collective-permute-start(f32[5,96]{1,0:T(8,128)S(1)} %pad_maximum_fusion.5), channel_id=1, source_target_pairs={{0,8},{2,10},{4,12},{6,14},{8,0},{10,2},{12,4},{14,6},{16,24},{18,... | collective-permute-start | bytes 5768 | tf_op jit(solution)/shard_map/ppermute | solution.py:14
  9.0 4.2 %collective-permute-start.3 = (f32[7,96]{1,0:T(8,128)S(1)}, f32[7,96]{1,0:T(8,128)S(1)}, u32[]{:S(2)}, u32[]{:S(2)}) collective-permute-start(f32[7,96]{1,0:T(8,128)S(1)} %pad_maximum_fusion.6), channel_id=1, source_target_pairs={{0,4},{2,6},{4,0},{6,2},{8,12},{10,14},{12,8},{14,10},{16,20},{18,... | collective-permute-start | bytes 8072 | tf_op jit(solution)/shard_map/ppermute | solution.py:14
  10.6 4.6 %collective-permute-start.1 = (f32[5,192]{1,0:T(8,128)S(1)}, f32[5,192]{1,0:T(8,128)S(1)}, u32[]{:S(2)}, u32[]{:S(2)}) collective-permute-start(f32[5,192]{1,0:T(8,128)S(1)} %pad_maximum_fusion.4), channel_id=1, source_target_pairs={{0,16},{2,18},{4,20},{6,22},{8,24},{10,26},{12,28},{14,30},{16,0},... | collective-permute-start | bytes 11528 | tf_op jit(solution)/shard_map/ppermute | solution.py:14
  13.3 1.9 %copy-start = (bf16[48,3,128]{2,0,1:T(8,128)(2,1)S(1)}, bf16[48,3,128]{2,0,1:T(8,128)(2,1)}, u32[]{:S(2)}) copy-start(bf16[48,3,128]{2,0,1:T(8,128)(2,1)} %param.23) | copy-start | bytes 110596
  15.2 4.4 %collective-permute-start.5 = (bf16[96,3,128]{2,0,1:T(8,128)(2,1)S(1)}, bf16[96,3,128]{2,0,1:T(8,128)(2,1)S(1)}, u32[]{:S(2)}, u32[]{:S(2)}) collective-permute-start(bf16[96,3,128]{2,0,1:T(8,128)(2,1)S(1)} %pad_maximum_fusion.1), channel_id=1, source_target_pairs={{0,4},{2,6},{4,0},{6,2},{8,12},{10,14},{12,8},{14,10},{16,20},{18,... | collective-permute-start | bytes 221192 | tf_op jit(solution)/shard_map/ppermute | solution.py:14
  23.1 5.6 %collective-permute-start.6 = (f32[192,128]{1,0:T(8,128)S(1)}, f32[192,128]{1,0:T(8,128)S(1)}, u32[]{:S(2)}, u32[]{:S(2)}) collective-permute-start(f32[192,128]{1,0:T(8,128)S(1)} %bitcast.102), channel_id=1, source_target_pairs={{0,16},{2,18},{4,20},{6,22},{8,24},{10,26},{12,28},{14,30},{16,0},... | collective-permute-start | bytes 294920 | tf_op jit(solution)/shard_map/ppermute | solution.py:14
  28.7 2.2 %copy-start.7 = (s32[96]{0:T(128)S(1)}, s32[96]{0:T(128)}, u32[]{:S(2)}) copy-start(s32[96]{0:T(128)} %param.17) | copy-start | bytes 1156
  28.8 4.3 %copy-start.4 = (f32[96]{0:T(128)S(1)}, f32[96]{0:T(128)}, u32[]{:S(2)}) copy-start(f32[96]{0:T(128)} %param.16) | copy-start | bytes 1156
  28.8 4.2 %copy-start.5 = (f32[96]{0:T(128)S(1)}, f32[96]{0:T(128)}, u32[]{:S(2)}) copy-start(f32[96]{0:T(128)} %param.15) | copy-start | bytes 1156
  28.8 4.2 %collective-permute-start.7 = (f32[96,128]{1,0:T(8,128)S(1)}, f32[96,128]{1,0:T(8,128)S(1)}, u32[]{:S(2)}, u32[]{:S(2)}) collective-permute-start(f32[96,128]{1,0:T(8,128)S(1)} %slice_select_fusion.2), channel_id=1, source_target_pairs={{0,8},{2,10},{4,12},{6,14},{8,0},{10,2},{12,4},{14,6},{16,24},{18,... | collective-permute-start | bytes 147464 | tf_op jit(solution)/shard_map/ppermute | solution.py:14
where the time goes:
time: 74.4 us; the launch traced here: 74.1 us
  blocking collectives  39.8 us (53%)
  starting transfers between devices  14.3 us (19%)
  waiting for transfers between devices  11.6 us (16%)
  other arithmetic  4.89 us (7%)
  local copies, waits for them, and re-layouts  1.55 us (2%)
  matrix products  0.95 us (1%)
  between operations  0.75 us (1%)
    psum x1, blocking collectives, per_device(): misfit = lax.psum(own_sum, ('patch', 'pix')) / pixels  39.8 us
    ppermute x8, starting transfers between devices, partner(): return lax.ppermute(value, axis, pairs)  14.3 us
    ppermute x8, waiting for transfers between devices, partner(): return lax.ppermute(value, axis, pairs)  11.6 us
    another operation x4, other arithmetic  2.11 us
  transfers between devices with their start and end apart: 8, of which 5 were waited for; matrix products, arithmetic and copies ran while one was open for 2% of the time, Pallas kernels for 0%

commit v1 on v0

--- a/solution.py
+++ b/solution.py
@@ -183,7 +183,7 @@
     )
     own_sum = jnp.sum(residual * residual, axis=0)
     pixels = own_pixels * lax.axis_size("patch") * lax.axis_size("pix")
-    misfit = lax.psum(own_sum, ("patch", "pix")) / pixels
+    misfit = jnp.sum(lax.all_gather(own_sum, ("patch", "pix")), axis=0) / pixels
     return (residual, misfit)
 
 

time: 74.4 us -> 76.2 us (1.024)
  blocking collectives: 39.8 us -> 41.7 us
    all_gather x0 -> x1, blocking collectives: none -> 41.7 us  [per_device(): misfit = jnp.sum(lax.all_gather(own_sum, ('patch', 'pix')), axis=0) / pixels]
    psum x1 -> x0, blocking collectives: 39.8 us -> none  [per_device(): misfit = lax.psum(own_sum, ('patch', 'pix')) / pixels]
where the time goes in v1:
time: 76.2 us; the launch traced here: 76 us
  blocking collectives  41.7 us (55%)
  starting transfers between devices  14.3 us (19%)
  waiting for transfers between devices  11.6 us (15%)
  other arithmetic  4.94 us (6%)
  local copies, waits for them, and re-layouts  1.55 us (2%)
  matrix products  0.95 us (1%)
    all_gather x1, blocking collectives, per_device(): misfit = jnp.sum(lax.all_gather(own_sum, ('patch', 'pix')), axis=0) / pixels  41.7 us
    ppermute x8, starting transfers between devices, partner(): return lax.ppermute(value, axis, pairs)  14.3 us
    ppermute x8, waiting for transfers between devices, partner(): return lax.ppermute(value, axis, pairs)  11.6 us
    another operation x4, other arithmetic  2.11 us
  transfers between devices with their start and end apart: 8, of which 5 were waited for; matrix products, arithmetic and copies ran while one was open for 2% of the time, Pallas kernels for 0%

profile of v1, /device:TPU:0, one launch (start us, length us, event | category | flops | bytes accessed | tf_op | source)
XLA Modules:
  0.0 76.0 jit_solution(5165784182554445836)
XLA Ops:
  0.6 3.0 %collective-permute-start.4 = (bf16[48,3,128]{2,0,1:T(8,128)(2,1)}, bf16[48,3,128]{2,0,1:T(8,128)(2,1)S(1)}, u32[]{:S(2)}, u32[]{:S(2)}) collective-permute-start(bf16[48,3,128]{2,0,1:T(8,128)(2,1)} %param.23), channel_id=1, source_target_pairs={{0,2},{2,0},{4,6},{6,4},{8,10},{10,8},{12,14},{14,12},{16,18},{18,... | collective-permute-start | bytes 110600 | tf_op jit(solution)/shard_map/ppermute | solution.py:14
  3.7 0.8 %select_reduce_fusion = (f32[48]{0:T(128)S(1)}, f32[48]{0:T(128)S(1)}) fusion(f32[16]{0:T(128)} %param.22, s32[48]{0:T(128)} %param.20, f32[16]{0:T(128)} %param.21), kind=kLoop, calls=%fused_computation.120 | loop fusion | flops 3744 | bytes 704 | tf_op jit(solution)/shard_map/reduce_sum | solution.py:80
  4.5 0.7 copy-done.3
  5.2 0.1 collective-permute-start.2
  5.3 0.6 copy-done.1
  5.9 1.6 %collective-permute-start = (f32[5,96]{1,0:T(8,128)S(1)}, f32[5,96]{1,0:T(8,128)S(1)}, u32[]{:S(2)}, u32[]{:S(2)}) collective-permute-start(f32[5,96]{1,0:T(8,128)S(1)} %pad_maximum_fusion.5), channel_id=1, source_target_pairs={{0,8},{2,10},{4,12},{6,14},{8,0},{10,2},{12,4},{14,6},{16,24},{18,... | collective-permute-start | bytes 5768 | tf_op jit(solution)/shard_map/ppermute | solution.py:14
  7.5 1.4 %collective-permute-done.2 = f32[7,48]{1,0:T(8,128)S(1)} collective-permute-done((f32[7,48]{1,0:T(8,128)S(1)}, f32[7,48]{1,0:T(8,128)S(1)}, u32[]{:S(2)}, u32[]{:S(2)}) %collective-permute-start.2) | collective-permute-done | bytes 1376 | tf_op jit(solution)/shard_map/ppermute | solution.py:14
  8.9 0.1 pad_maximum_fusion.6
  9.0 1.5 %collective-permute-start.3 = (f32[7,96]{1,0:T(8,128)S(1)}, f32[7,96]{1,0:T(8,128)S(1)}, u32[]{:S(2)}, u32[]{:S(2)}) collective-permute-start(f32[7,96]{1,0:T(8,128)S(1)} %pad_maximum_fusion.6), channel_id=1, source_target_pairs={{0,4},{2,6},{4,0},{6,2},{8,12},{10,14},{12,8},{14,10},{16,20},{18,... | collective-permute-start | bytes 8072 | tf_op jit(solution)/shard_map/ppermute | solution.py:14
  10.6 2.6 %collective-permute-start.1 = (f32[5,192]{1,0:T(8,128)S(1)}, f32[5,192]{1,0:T(8,128)S(1)}, u32[]{:S(2)}, u32[]{:S(2)}) collective-permute-start(f32[5,192]{1,0:T(8,128)S(1)} %pad_maximum_fusion.4), channel_id=1, source_target_pairs={{0,16},{2,18},{4,20},{6,22},{8,24},{10,26},{12,28},{14,30},{16,0},... | collective-permute-start | bytes 11528 | tf_op jit(solution)/shard_map/ppermute | solution.py:14
  13.2 0.1 multiply_bitcast_fusion
  13.3 0.1 multiply_bitcast_fusion.1
  13.5 1.6 %collective-permute-done.1 = f32[5,192]{1,0:T(8,128)S(1)} collective-permute-done((f32[5,192]{1,0:T(8,128)S(1)}, f32[5,192]{1,0:T(8,128)S(1)}, u32[]{:S(2)}, u32[]{:S(2)}) %collective-permute-start.1) | collective-permute-done | bytes 3872 | tf_op jit(solution)/shard_map/ppermute | solution.py:14
  15.2 0.7 collective-permute-start.5
  16.0 0.1 reshape.2726
  16.0 3.6 %collective-permute-done.5 = bf16[96,3,128]{2,0,1:T(8,128)(2,1)S(1)} collective-permute-done((bf16[96,3,128]{2,0,1:T(8,128)(2,1)S(1)}, bf16[96,3,128]{2,0,1:T(8,128)(2,1)S(1)}, u32[]{:S(2)}, u32[]{:S(2)}) %collective-permute-start.5) | collective-permute-done | bytes 73760 | tf_op jit(solution)/shard_map/ppermute | solution.py:14
  19.7 3.4 %while.11 = (s32[]{:T(128)}, f32[4,96,128]{2,1,0:T(8,128)S(1)}, f32[4,5,96]{2,0,1:T(4,128)S(1)}, f32[7,192]{1,0:T(8,128)S(1)}, f32[192,1]{0,1:T(1,128)S(1)}, /*i...) while((s32[]{:T(128)}, f32[4,96,128]{2,1,0:T(8,128)S(1)}, ...), condition=%wide.region_3.4_spmd, body=%wide.region_2.3_spmd.sunk | while | flops 16626054 | bytes 485213 | solution.py:172
  19.8 0.5 fusion.98
  20.3 0.2 fusion.99
  20.6 0.5 fusion.98
  21.2 0.2 fusion.99
  21.5 0.5 fusion.98
  22.0 0.2 fusion.99
  22.3 0.5 fusion.98
  22.9 0.2 fusion.99
  23.1 2.7 %collective-permute-start.6 = (f32[192,128]{1,0:T(8,128)S(1)}, f32[192,128]{1,0:T(8,128)S(1)}, u32[]{:S(2)}, u32[]{:S(2)}) collective-permute-start(f32[192,128]{1,0:T(8,128)S(1)} %bitcast.103), channel_id=1, source_target_pairs={{0,16},{2,18},{4,20},{6,22},{8,24},{10,26},{12,28},{14,30},{16,0},... | collective-permute-start | bytes 294920 | tf_op jit(solution)/shard_map/ppermute | solution.py:14
  25.8 2.9 %collective-permute-done.6 = f32[192,128]{1,0:T(8,128)S(1)} collective-permute-done((f32[192,128]{1,0:T(8,128)S(1)}, f32[192,128]{1,0:T(8,128)S(1)}, u32[]{:S(2)}, u32[]{:S(2)}) %collective-permute-start.6) | collective-permute-done | bytes 98336 | tf_op jit(solution)/shard_map/ppermute | solution.py:14
  28.8 2.2 %collective-permute-start.7 = (f32[96,128]{1,0:T(8,128)S(1)}, f32[96,128]{1,0:T(8,128)S(1)}, u32[]{:S(2)}, u32[]{:S(2)}) collective-permute-start(f32[96,128]{1,0:T(8,128)S(1)} %slice_select_fusion.2), channel_id=1, source_target_pairs={{0,8},{2,10},{4,12},{6,14},{8,0},{10,2},{12,4},{14,6},{16,24},{18,... | collective-permute-start | bytes 147464 | tf_op jit(solution)/shard_map/ppermute | solution.py:14
  31.0 2.1 %collective-permute-done.7 = f32[96,128]{1,0:T(8,128)S(1)} collective-permute-done((f32[96,128]{1,0:T(8,128)S(1)}, f32[96,128]{1,0:T(8,128)S(1)}, u32[]{:S(2)}, u32[]{:S(2)}) %collective-permute-start.7) | collective-permute-done | bytes 49184 | tf_op jit(solution)/shard_map/ppermute | solution.py:14
  33.0 0.7 multiply_reduce_fusion
  33.8 41.7 %all-gather.1 = f32[32,1,128]{2,1,0:T(1,128)S(1)} all-gather(f32[1,1,128]{2,1,0:T(1,128)S(1)} %bitcast.108), channel_id=2, replica_groups=mesh['patch'=16,'pix'=2] {'patch','pix'}, dimensions={0}, use_global_device_ids=true | all-gather | bytes 16896 | tf_op jit(solution)/shard_map/all_gather | solution.py:186
  75.5 0.5 broadcast_multiply_fusion.2
  (50 shorter events, 0.8 us)
Async XLA Ops:
  0.6 14.6 %collective-permute-start.4 = (bf16[48,3,128]{2,0,1:T(8,128)(2,1)}, bf16[48,3,128]{2,0,1:T(8,128)(2,1)S(1)}, u32[]{:S(2)}, u32[]{:S(2)}) collective-permute-start(bf16[48,3,128]{2,0,1:T(8,128)(2,1)} %param.23), channel_id=1, source_target_pairs={{0,2},{2,0},{4,6},{6,4},{8,10},{10,8},{12,14},{14,12},{16,18},{18,... | collective-permute-start | bytes 110600 | tf_op jit(solution)/shard_map/ppermute | solution.py:14
  4.5 0.7 copy-start.3
  4.5 0.7 copy-start.6
  5.2 0.7 copy-start.1
  5.2 0.7 copy-start.2
  5.2 3.7 %collective-permute-start.2 = (f32[7,48]{1,0:T(8,128)S(1)}, f32[7,48]{1,0:T(8,128)S(1)}, u32[]{:S(2)}, u32[]{:S(2)}) collective-permute-start(f32[7,48]{1,0:T(8,128)S(1)} %stack.24), channel_id=1, source_target_pairs={{0,2},{2,0},{4,6},{6,4},{8,10},{10,8},{12,14},{14,12},{16,18},{18,... | collective-permute-start | bytes 4040 | tf_op jit(solution)/shard_map/ppermute | solution.py:14
  5.9 4.6 %collective-permute-start = (f32[5,96]{1,0:T(8,128)S(1)}, f32[5,96]{1,0:T(8,128)S(1)}, u32[]{:S(2)}, u32[]{:S(2)}) collective-permute-start(f32[5,96]{1,0:T(8,128)S(1)} %pad_maximum_fusion.5), channel_id=1, source_target_pairs={{0,8},{2,10},{4,12},{6,14},{8,0},{10,2},{12,4},{14,6},{16,24},{18,... | collective-permute-start | bytes 5768 | tf_op jit(solution)/shard_map/ppermute | solution.py:14
  9.0 4.2 %collective-permute-start.3 = (f32[7,96]{1,0:T(8,128)S(1)}, f32[7,96]{1,0:T(8,128)S(1)}, u32[]{:S(2)}, u32[]{:S(2)}) collective-permute-start(f32[7,96]{1,0:T(8,128)S(1)} %pad_maximum_fusion.6), channel_id=1, source_target_pairs={{0,4},{2,6},{4,0},{6,2},{8,12},{10,14},{12,8},{14,10},{16,20},{18,... | collective-permute-start | bytes 8072 | tf_op jit(solution)/shard_map/ppermute | solution.py:14
  10.6 4.6 %collective-permute-start.1 = (f32[5,192]{1,0:T(8,128)S(1)}, f32[5,192]{1,0:T(8,128)S(1)}, u32[]{:S(2)}, u32[]{:S(2)}) collective-permute-start(f32[5,192]{1,0:T(8,128)S(1)} %pad_maximum_fusion.4), channel_id=1, source_target_pairs={{0,16},{2,18},{4,20},{6,22},{8,24},{10,26},{12,28},{14,30},{16,0},... | collective-permute-start | bytes 11528 | tf_op jit(solution)/shard_map/ppermute | solution.py:14
  13.3 1.9 %copy-start = (bf16[48,3,128]{2,0,1:T(8,128)(2,1)S(1)}, bf16[48,3,128]{2,0,1:T(8,128)(2,1)}, u32[]{:S(2)}) copy-start(bf16[48,3,128]{2,0,1:T(8,128)(2,1)} %param.23) | copy-start | bytes 110596
  15.2 4.4 %collective-permute-start.5 = (bf16[96,3,128]{2,0,1:T(8,128)(2,1)S(1)}, bf16[96,3,128]{2,0,1:T(8,128)(2,1)S(1)}, u32[]{:S(2)}, u32[]{:S(2)}) collective-permute-start(bf16[96,3,128]{2,0,1:T(8,128)(2,1)S(1)} %pad_maximum_fusion.1), channel_id=1, source_target_pairs={{0,4},{2,6},{4,0},{6,2},{8,12},{10,14},{12,8},{14,10},{16,20},{18,... | collective-permute-start | bytes 221192 | tf_op jit(solution)/shard_map/ppermute | solution.py:14
  23.1 5.6 %collective-permute-start.6 = (f32[192,128]{1,0:T(8,128)S(1)}, f32[192,128]{1,0:T(8,128)S(1)}, u32[]{:S(2)}, u32[]{:S(2)}) collective-permute-start(f32[192,128]{1,0:T(8,128)S(1)} %bitcast.103), channel_id=1, source_target_pairs={{0,16},{2,18},{4,20},{6,22},{8,24},{10,26},{12,28},{14,30},{16,0},... | collective-permute-start | bytes 294920 | tf_op jit(solution)/shard_map/ppermute | solution.py:14
  28.7 2.2 %copy-start.7 = (s32[96]{0:T(128)S(1)}, s32[96]{0:T(128)}, u32[]{:S(2)}) copy-start(s32[96]{0:T(128)} %param.17) | copy-start | bytes 1156
  28.8 4.3 %copy-start.4 = (f32[96]{0:T(128)S(1)}, f32[96]{0:T(128)}, u32[]{:S(2)}) copy-start(f32[96]{0:T(128)} %param.16) | copy-start | bytes 1156
  28.8 4.2 %copy-start.5 = (f32[96]{0:T(128)S(1)}, f32[96]{0:T(128)}, u32[]{:S(2)}) copy-start(f32[96]{0:T(128)} %param.15) | copy-start | bytes 1156
  28.8 4.2 %collective-permute-start.7 = (f32[96,128]{1,0:T(8,128)S(1)}, f32[96,128]{1,0:T(8,128)S(1)}, u32[]{:S(2)}, u32[]{:S(2)}) collective-permute-start(f32[96,128]{1,0:T(8,128)S(1)} %slice_select_fusion.2), channel_id=1, source_target_pairs={{0,8},{2,10},{4,12},{6,14},{8,0},{10,2},{12,4},{14,6},{16,24},{18,... | collective-permute-start | bytes 147464 | tf_op jit(solution)/shard_map/ppermute | solution.py:14
